TPU v7x, 32 devices: a whole 2x2x4 slice. The times are simulated.
32 devices in a mesh: rows: 16 (over z, y, core), cols: 2 (over x).
Axes of the slice: x: 2, y: 2, z: 4, core: 2. Of those that a mesh axis runs over, the one named last changes fastest.
Arguments:
- design: bfloat16 [32768, 6144], P('rows', 'cols'), may hold values from -0.03125 to 0.03125
- targets: bfloat16 [32768, 128], P('rows'), may hold values from -6 to 6
- col_scale: float32 [6144], P('cols'), may hold values from 0.1 to 1
Outputs:
- solution: float32 [6144, 128], P('cols', 'rows')
- residual: float32 [32768, 128], P('rows')
All inputs are finite; a program needn't handle non-finite values.
Results may differ from a plain program's by a relative error of at most 0.0065.
Values may be sent and summed in bfloat16 or wider, within the bound.
A program may use at most 128 MiB of HBM per device.

v0:
```python
import jax
import jax.numpy as jnp
from jax import lax
from jax.sharding import PartitionSpec as P

ITERS = 6


def local_back(design, vectors):
    return lax.dot_general(
        design, vectors, (((0,), (0,)), ((), ())), preferred_element_type=jnp.float32
    )


def per_device(design, targets, col_scale):
    fits = targets.shape[1]
    row_count = lax.axis_size("rows")
    residual = targets.astype(jnp.float32)
    scale = col_scale[:, None]

    def gradient_of(vectors):
        return scale * lax.psum(local_back(design, vectors), "rows")

    def squared(values):
        return lax.psum(jnp.sum(values * values, axis=0), "cols")

    gradient = gradient_of(targets)
    gamma = squared(gradient)
    solution = jnp.zeros(gradient.shape, jnp.float32)
    direction = gradient
    for step in range(ITERS):
        scaled_dir = (scale * direction).astype(jnp.bfloat16)
        image = lax.psum(
            jnp.dot(design, scaled_dir, preferred_element_type=jnp.float32).astype(jnp.bfloat16),
            "cols",
        ).astype(jnp.float32)
        delta = lax.psum(jnp.sum(image * image, axis=0), "rows")
        alpha = gamma / delta
        solution = solution + alpha * direction
        residual = residual - alpha * image
        if step + 1 < ITERS:
            gradient = gradient_of(residual.astype(jnp.bfloat16))
            gamma_new = squared(gradient)
            direction = gradient + gamma_new / gamma * direction
            gamma = gamma_new
    own = fits // row_count
    solution_part = lax.dynamic_slice_in_dim(solution, lax.axis_index("rows") * own, own, 1)
    return (solution_part, residual)


def solution(mesh):
    in_specs = (P("rows", "cols"), P("rows", None), P("cols"))
    out_specs = (P("cols", "rows"), P("rows", None))
    return jax.shard_map(
        per_device, mesh=mesh, in_specs=in_specs, out_specs=out_specs, check_vma=False
    )
```

profile of v0, /device:TPU:0, one launch (start us, length us, event | category | flops | bytes accessed | tf_op | source)
XLA Modules:
  0.0 1142.6 jit_solution(10677562298321157389)
XLA Ops:
  7.2 9.3 fusion.42
  16.5 98.8 %all-reduce.13.cloned.1.call-done = f32[3072,128]{1,0:T(8,128)} async-done(((f32[3072,128]{1,0:T(8,128)}), f32[3072,128]{1,0:T(8,128)}) %all-reduce.13.cloned.1.call-update) | async-done | bytes 1572880 | tf_op jit(solution)/shard_map/psum | solution.py:22
  115.3 1.9 multiply_reduce_fusion.5
  117.2 10.4 fusion
  127.9 4.9 psum.169
  132.8 22.5 %all-reduce.15.cloned.1.call-done = bf16[2048,128]{0,1:T(8,128)(2,1)} async-done(((bf16[2048,128]{0,1:T(8,128)(2,1)}), bf16[2048,128]{0,1:T(8,128)(2,1)}) %all-reduce.15.cloned.1.call-update) | async-done | bytes 524304 | tf_op jit(solution)/shard_map/psum | solution.py:33
  156.5 33.2 %psum.171 = f32[128]{0:T(128)S(1)} all-reduce(f32[128]{0:T(128)S(1)} %fusion.11), channel_id=1, replica_groups=mesh['rows'=16,'cols'=2] {'rows'}, use_global_device_ids=true, to_apply=%region_5.0 | all-reduce | flops 128 | bytes 1024 | tf_op jit(solution)/shard_map/psum | solution.py:37
  189.8 11.0 convolution_bitcast_fusion.4
  200.8 92.3 %all-reduce.17.cloned.1.call-done = f32[3072,128]{1,0:T(8,128)} async-done(((f32[3072,128]{1,0:T(8,128)}), f32[3072,128]{1,0:T(8,128)}) %all-reduce.17.cloned.1.call-update) | async-done | bytes 1572880 | tf_op jit(solution)/shard_map/psum | solution.py:22
  293.1 1.9 multiply_reduce_fusion.4
  295.0 4.9 psum.173
  301.9 10.3 fusion.1
  312.2 27.6 %all-reduce.19.cloned.1.call-done = bf16[2048,128]{0,1:T(8,128)(2,1)} async-done(((bf16[2048,128]{0,1:T(8,128)(2,1)}), bf16[2048,128]{0,1:T(8,128)(2,1)}) %all-reduce.19.cloned.1.call-update) | async-done | bytes 524304 | tf_op jit(solution)/shard_map/psum | solution.py:33
  341.1 33.4 %psum.175 = f32[128]{0:T(128)S(1)} all-reduce(f32[128]{0:T(128)S(1)} %fusion.13), channel_id=1, replica_groups=mesh['rows'=16,'cols'=2] {'rows'}, use_global_device_ids=true, to_apply=%region_11.0 | all-reduce | flops 128 | bytes 1024 | tf_op jit(solution)/shard_map/psum | solution.py:37
  374.5 11.3 convolution_bitcast_fusion.3
  385.9 92.3 %all-reduce.21.cloned.1.call-done = f32[3072,128]{1,0:T(8,128)} async-done(((f32[3072,128]{1,0:T(8,128)}), f32[3072,128]{1,0:T(8,128)}) %all-reduce.21.cloned.1.call-update) | async-done | bytes 1572880 | tf_op jit(solution)/shard_map/psum | solution.py:22
  478.3 1.9 multiply_reduce_fusion.3
  480.2 4.9 psum.177
  488.1 10.3 fusion.2
  498.5 27.6 %all-reduce.23.cloned.1.call-done = bf16[2048,128]{0,1:T(8,128)(2,1)} async-done(((bf16[2048,128]{0,1:T(8,128)(2,1)}), bf16[2048,128]{0,1:T(8,128)(2,1)}) %all-reduce.23.cloned.1.call-update) | async-done | bytes 524304 | tf_op jit(solution)/shard_map/psum | solution.py:33
  527.4 33.2 %psum.179 = f32[128]{0:T(128)S(1)} all-reduce(f32[128]{0:T(128)S(1)} %fusion.15), channel_id=1, replica_groups=mesh['rows'=16,'cols'=2] {'rows'}, use_global_device_ids=true, to_apply=%region_17.0 | all-reduce | flops 128 | bytes 1024 | tf_op jit(solution)/shard_map/psum | solution.py:37
  560.6 11.5 %convolution_bitcast_fusion.2 = f32[3072,128]{1,0:T(8,128)} fusion(bf16[2048,3072]{1,0:T(8,128)(2,1)} %param.3, bf16[2048,128]{0,1:T(8,128)(2,1)} %all-reduce.23.cloned.1.call-done, f32[128]{0:T(128)S(1)} %div.37, bf16[2048,128]{0,1:T(8,128)(2,1)} %all-reduce.19.cloned.1.call-done, bf16[2048,128]{0,1:T(8,128)(2,1)} %all-reduce.15.cloned.1.call-done, ...), kind=kOutput, calls=%fused_computation.2 | convolution fusion | flops 1613496320 | bytes 16254464 | tf_op jit(solution)/shard_map/dot_general | solution.py:10
  572.2 92.0 %all-reduce.25.cloned.1.call-done = f32[3072,128]{1,0:T(8,128)} async-done(((f32[3072,128]{1,0:T(8,128)}), f32[3072,128]{1,0:T(8,128)}) %all-reduce.25.cloned.1.call-update) | async-done | bytes 1572880 | tf_op jit(solution)/shard_map/psum | solution.py:22
  664.2 1.9 multiply_reduce_fusion.2
  666.1 4.9 psum.181
  671.0 2.4 multiply_add_fusion.2
  674.5 10.3 fusion.3
  684.9 27.6 %all-reduce.27.cloned.1.call-done = bf16[2048,128]{0,1:T(8,128)(2,1)} async-done(((bf16[2048,128]{0,1:T(8,128)(2,1)}), bf16[2048,128]{0,1:T(8,128)(2,1)}) %all-reduce.27.cloned.1.call-update) | async-done | bytes 524304 | tf_op jit(solution)/shard_map/psum | solution.py:33
  713.8 33.2 %psum.183 = f32[128]{0:T(128)S(1)} all-reduce(f32[128]{0:T(128)S(1)} %fusion.17), channel_id=1, replica_groups=mesh['rows'=16,'cols'=2] {'rows'}, use_global_device_ids=true, to_apply=%region_23.0 | all-reduce | flops 128 | bytes 1024 | tf_op jit(solution)/shard_map/psum | solution.py:37
  747.0 2.3 fusion.18
  750.3 9.1 convolution_bitcast_fusion.1
  759.4 92.2 %all-reduce.29.cloned.1.call-done = f32[3072,128]{1,0:T(8,128)} async-done(((f32[3072,128]{1,0:T(8,128)}), f32[3072,128]{1,0:T(8,128)}) %all-reduce.29.cloned.1.call-update) | async-done | bytes 1572880 | tf_op jit(solution)/shard_map/psum | solution.py:22
  853.5 4.9 psum.185
  858.4 2.4 multiply_add_fusion.1
  861.9 10.3 fusion.4
  872.3 27.6 %all-reduce.31.cloned.1.call-done = bf16[2048,128]{0,1:T(8,128)(2,1)} async-done(((bf16[2048,128]{0,1:T(8,128)(2,1)}), bf16[2048,128]{0,1:T(8,128)(2,1)}) %all-reduce.31.cloned.1.call-update) | async-done | bytes 524304 | tf_op jit(solution)/shard_map/psum | solution.py:33
  901.2 33.3 %psum.187 = f32[128]{0:T(128)S(1)} all-reduce(f32[128]{0:T(128)S(1)} %fusion.19), channel_id=1, replica_groups=mesh['rows'=16,'cols'=2] {'rows'}, use_global_device_ids=true, to_apply=%region_29.0 | all-reduce | flops 128 | bytes 1024 | tf_op jit(solution)/shard_map/psum | solution.py:37
  934.5 11.3 convolution_bitcast_fusion
  945.8 92.0 %all-reduce.33.cloned.1.call-done = f32[3072,128]{1,0:T(8,128)} async-done(((f32[3072,128]{1,0:T(8,128)}), f32[3072,128]{1,0:T(8,128)}) %all-reduce.33.cloned.1.call-update) | async-done | bytes 1572880 | tf_op jit(solution)/shard_map/psum | solution.py:22
  1039.7 4.9 psum.189
  1044.7 2.4 multiply_add_fusion
  1048.2 10.3 fusion.5
  1058.9 27.3 %all-reduce.35.cloned.1.call-done = bf16[2048,128]{0,1:T(8,128)(2,1)} async-done(((bf16[2048,128]{0,1:T(8,128)(2,1)}), bf16[2048,128]{0,1:T(8,128)(2,1)}) %all-reduce.35.cloned.1.call-update) | async-done | bytes 524304 | tf_op jit(solution)/shard_map/psum | solution.py:33
  1087.5 33.3 %psum.191 = f32[128]{0:T(128)S(1)} all-reduce(f32[128]{0:T(128)S(1)} %fusion.21), channel_id=1, replica_groups=mesh['rows'=16,'cols'=2] {'rows'}, use_global_device_ids=true, to_apply=%region_35.0 | all-reduce | flops 128 | bytes 1024 | tf_op jit(solution)/shard_map/psum | solution.py:37
  1120.9 2.8 fusion.22
  1123.7 2.5 copy.12
  1126.3 6.5 fusion.6
  1132.7 2.5 copy.11
  (68 shorter events, 21.9 us)
Async XLA Ops:
  7.2 108.2 %all-reduce.13.cloned.1.call-start = ((), (), s32[]{:S(2)}) async-start(), calls=%async_computation | async-start | bytes 3145728 | tf_op jit(solution)/shard_map/psum | solution.py:22
  16.5 98.9 %copy-start.6 = (f32[3072]{0:T(1024)S(1)}, f32[3072]{0:T(1024)}, u32[]{:S(2)}) copy-start(f32[3072]{0:T(1024)} %param.5) | copy-start | bytes 36868
  16.5 138.8 %all-reduce.15.cloned.1.call-start = ((), (), s32[]{:S(2)}) async-start(), calls=%async_computation.1 | async-start | bytes 1048576 | tf_op jit(solution)/shard_map/psum | solution.py:33
  117.2 10.4 copy-start.7
  127.6 165.5 %all-reduce.17.cloned.1.call-start = ((), (), s32[]{:S(2)}) async-start(), calls=%async_computation.2 | async-start | bytes 3145728 | tf_op jit(solution)/shard_map/psum | solution.py:22
  127.9 72.8 %copy-start.5 = (bf16[2048,128]{0,1:T(8,128)(2,1)}, bf16[2048,128]{0,1:T(8,128)(2,1)S(1)}, u32[]{:S(2)}) copy-start(bf16[2048,128]{0,1:T(8,128)(2,1)S(1)} %copy.5) | copy-start | bytes 1572868
  200.7 139.1 %all-reduce.19.cloned.1.call-start = ((), (), s32[]{:S(2)}) async-start(), calls=%async_computation.3 | async-start | bytes 1048576 | tf_op jit(solution)/shard_map/psum | solution.py:33
  312.2 166.1 %all-reduce.21.cloned.1.call-start = ((), (), s32[]{:S(2)}) async-start(), calls=%async_computation.4 | async-start | bytes 3145728 | tf_op jit(solution)/shard_map/psum | solution.py:22
  385.9 140.3 %all-reduce.23.cloned.1.call-start = ((), (), s32[]{:S(2)}) async-start(), calls=%async_computation.5 | async-start | bytes 1048576 | tf_op jit(solution)/shard_map/psum | solution.py:33
  487.0 1.2 copy-start
  498.5 165.7 %all-reduce.25.cloned.1.call-start = ((), (), s32[]{:S(2)}) async-start(), calls=%async_computation.6 | async-start | bytes 3145728 | tf_op jit(solution)/shard_map/psum | solution.py:22
  572.1 140.4 %all-reduce.27.cloned.1.call-start = ((), (), s32[]{:S(2)}) async-start(), calls=%async_computation.7 | async-start | bytes 1048576 | tf_op jit(solution)/shard_map/psum | solution.py:33
  673.4 1.1 copy-start.1
  684.9 166.7 %all-reduce.29.cloned.1.call-start = ((), (), s32[]{:S(2)}) async-start(), calls=%async_computation.8 | async-start | bytes 3145728 | tf_op jit(solution)/shard_map/psum | solution.py:22
  749.3 1.0 copy-start.3
  759.4 140.6 %all-reduce.31.cloned.1.call-start = ((), (), s32[]{:S(2)}) async-start(), calls=%async_computation.9 | async-start | bytes 1048576 | tf_op jit(solution)/shard_map/psum | solution.py:33
  860.8 1.1 copy-start.2
  872.3 165.6 %all-reduce.33.cloned.1.call-start = ((), (), s32[]{:S(2)}) async-start(), calls=%async_computation.10 | async-start | bytes 3145728 | tf_op jit(solution)/shard_map/psum | solution.py:22
  945.7 140.5 %all-reduce.35.cloned.1.call-start = ((), (), s32[]{:S(2)}) async-start(), calls=%async_computation.11 | async-start | bytes 1048576 | tf_op jit(solution)/shard_map/psum | solution.py:33
  1047.0 1.2 copy-start.4
Sparse Core Ops, SparseCore 0:
  16.6 98.6 all-reduce.12
  127.7 27.5 all-reduce.14
  200.9 92.2 all-reduce.16
  312.3 27.5 all-reduce.18
  386.0 92.2 all-reduce.20
  498.6 27.5 all-reduce.22
  572.2 91.9 all-reduce.24
  685.0 27.5 all-reduce.26
  759.5 92.0 all-reduce.28
  872.4 27.5 all-reduce.30
  945.9 91.9 all-reduce.32
  1058.7 27.5 all-reduce.34
where the time goes:
time: 1150 us; the launch traced here: 1140 us
  waiting for transfers between devices  720 us (63%)
  blocking collectives  229 us (20%)
  matrix products  125 us (11%)
  other arithmetic  41.2 us (4%)
  between operations  14.8 us (1%)
    psum x6, waiting for transfers between devices, gradient_of(): return scale * lax.psum(local_back(design, vectors), 'rows')  560 us
    psum x6, blocking collectives, per_device(): delta = lax.psum(jnp.sum(image * image, axis=0), 'rows')  200 us
    psum x6, waiting for transfers between devices, per_device(): lax.psum(jnp.dot(design, scaled_dir, preferred_element_type=jnp.float32)....  160 us
    dot_general x6, matrix products, local_back(): lax.dot_general(design, vectors, (((0,), (0,)), ((), ())), preferred_elem...  63.3 us
    dot_general x6, matrix products, per_device(): jnp.dot(design, scaled_dir, preferred_element_type=jnp.float32)  61.9 us
    psum x6, blocking collectives, squared(): return lax.psum(jnp.sum(values * values, axis=0), 'cols')  29.6 us
  transfers between devices with their start and end apart: 12, of which 12 were waited for; matrix products, arithmetic and copies ran while one was open for 0% of the time, Pallas kernels for 0%

commit v1 on v0

--- a/solution.py
+++ b/solution.py
@@ -34,7 +34,7 @@
             jnp.dot(design, scaled_dir, preferred_element_type=jnp.float32).astype(jnp.bfloat16),
             "cols",
         ).astype(jnp.float32)
-        delta = lax.psum(jnp.sum(image * image, axis=0), "rows")
+        delta = jnp.sum(lax.all_gather(jnp.sum(image * image, axis=0), "rows"), axis=0)
         alpha = gamma / delta
         solution = solution + alpha * direction
         residual = residual - alpha * image

time: 1150 us -> 1080 us (0.939)
  blocking collectives: 229 us -> 159 us
    psum x6 -> x0, blocking collectives: 200 us -> none  [per_device(): delta = lax.psum(jnp.sum(image * image, axis=0), 'rows')]
    all_gather x0 -> x6, blocking collectives: none -> 130 us  [per_device(): lax.all_gather(jnp.sum(image * image, axis=0), 'rows')]
where the time goes in v1:
time: 1080 us; the launch traced here: 1070 us
  waiting for transfers between devices  721 us (67%)
  blocking collectives  159 us (15%)
  matrix products  125 us (12%)
  other arithmetic  41.4 us (4%)
  between operations  14.8 us (1%)
  local copies, waits for them, and re-layouts  11.2 us (1%)
    psum x6, waiting for transfers between devices, gradient_of(): return scale * lax.psum(local_back(design, vectors), 'rows')  560 us
    psum x6, waiting for transfers between devices, per_device(): lax.psum(jnp.dot(design, scaled_dir, preferred_element_type=jnp.float32)....  160 us
    all_gather x6, blocking collectives, per_device(): lax.all_gather(jnp.sum(image * image, axis=0), 'rows')  130 us
    dot_general x6, matrix products, local_back(): lax.dot_general(design, vectors, (((0,), (0,)), ((), ())), preferred_elem...  63.3 us
    dot_general x6, matrix products, per_device(): jnp.dot(design, scaled_dir, preferred_element_type=jnp.float32)  61.9 us
    psum x6, blocking collectives, squared(): return lax.psum(jnp.sum(values * values, axis=0), 'cols')  29.6 us
  transfers between devices with their start and end apart: 12, of which 12 were waited for; matrix products, arithmetic and copies ran while one was open for 0% of the time, Pallas kernels for 0%

profile of v1, /device:TPU:0, one launch (start us, length us, event | category | flops | bytes accessed | tf_op | source)
XLA Modules:
  0.0 1072.9 jit_solution(10363548127557364346)
XLA Ops:
  7.2 9.3 fusion.42
  16.5 98.8 %all-reduce.13.cloned.1.call-done = f32[3072,128]{1,0:T(8,128)} async-done(((f32[3072,128]{1,0:T(8,128)}), f32[3072,128]{1,0:T(8,128)}) %all-reduce.13.cloned.1.call-update) | async-done | bytes 1572880 | tf_op jit(solution)/shard_map/psum | solution.py:22
  115.3 1.9 multiply_reduce_fusion.5
  117.2 10.4 fusion
  127.9 4.9 psum.127
  132.8 22.5 %all-reduce.15.cloned.1.call-done = bf16[2048,128]{0,1:T(8,128)(2,1)} async-done(((bf16[2048,128]{0,1:T(8,128)(2,1)}), bf16[2048,128]{0,1:T(8,128)(2,1)}) %all-reduce.15.cloned.1.call-update) | async-done | bytes 524304 | tf_op jit(solution)/shard_map/psum | solution.py:33
  156.5 21.5 %all-gather.6 = f32[16,1,128]{2,1,0:T(1,128)S(1)} all-gather(f32[1,1,128]{2,1,0:T(1,128)S(1)} %bitcast.41), channel_id=2, replica_groups=mesh['rows'=16,'cols'=2] {'rows'}, dimensions={0}, use_global_device_ids=true | all-gather | bytes 8704 | tf_op jit(solution)/shard_map/all_gather | solution.py:37
  178.1 11.0 %convolution_bitcast_fusion.4 = f32[3072,128]{1,0:T(8,128)} fusion(bf16[2048,3072]{1,0:T(8,128)(2,1)} %param.3, bf16[2048,128]{0,1:T(8,128)(2,1)} %all-reduce.15.cloned.1.call-done, bf16[2048,128]{0,1:T(8,128)(2,1)S(1)} %copy.13, f32[128]{0:T(128)S(1)} %div.33), kind=kOutput, calls=%fused_computation.4 | convolution fusion | flops 1611923456 | bytes 15204864 | tf_op jit(solution)/shard_map/dot_general | solution.py:10
  189.1 92.4 %all-reduce.17.cloned.1.call-done = f32[3072,128]{1,0:T(8,128)} async-done(((f32[3072,128]{1,0:T(8,128)}), f32[3072,128]{1,0:T(8,128)}) %all-reduce.17.cloned.1.call-update) | async-done | bytes 1572880 | tf_op jit(solution)/shard_map/psum | solution.py:22
  281.5 1.9 multiply_reduce_fusion.4
  283.4 4.9 psum.130
  290.2 10.3 fusion.1
  300.6 27.6 %all-reduce.19.cloned.1.call-done = bf16[2048,128]{0,1:T(8,128)(2,1)} async-done(((bf16[2048,128]{0,1:T(8,128)(2,1)}), bf16[2048,128]{0,1:T(8,128)(2,1)}) %all-reduce.19.cloned.1.call-update) | async-done | bytes 524304 | tf_op jit(solution)/shard_map/psum | solution.py:33
  329.5 21.7 %all-gather.7 = f32[16,1,128]{2,1,0:T(1,128)S(1)} all-gather(f32[1,1,128]{2,1,0:T(1,128)S(1)} %bitcast.42), channel_id=3, replica_groups=mesh['rows'=16,'cols'=2] {'rows'}, dimensions={0}, use_global_device_ids=true | all-gather | bytes 8704 | tf_op jit(solution)/shard_map/all_gather | solution.py:37
  351.3 11.3 %convolution_bitcast_fusion.3 = f32[3072,128]{1,0:T(8,128)} fusion(bf16[2048,3072]{1,0:T(8,128)(2,1)} %param.3, bf16[2048,128]{0,1:T(8,128)(2,1)} %all-reduce.19.cloned.1.call-done, bf16[2048,128]{0,1:T(8,128)(2,1)} %all-reduce.15.cloned.1.call-done, bf16[2048,128]{0,1:T(8,128)(2,1)} %copy-done.5, f32[128]{0:T(128)S(1)} %div.35, f32[128]{0:T(128)S(1)} %div.33), kind=kOutput, calls=%fused_computation.3 | convolution fusion | flops 1612709888 | bytes 15729664 | tf_op jit(solution)/shard_map/dot_general | solution.py:10
  362.6 92.4 %all-reduce.21.cloned.1.call-done = f32[3072,128]{1,0:T(8,128)} async-done(((f32[3072,128]{1,0:T(8,128)}), f32[3072,128]{1,0:T(8,128)}) %all-reduce.21.cloned.1.call-update) | async-done | bytes 1572880 | tf_op jit(solution)/shard_map/psum | solution.py:22
  455.0 1.9 multiply_reduce_fusion.3
  456.9 4.9 psum.133
  464.9 10.3 fusion.2
  475.2 27.6 %all-reduce.23.cloned.1.call-done = bf16[2048,128]{0,1:T(8,128)(2,1)} async-done(((bf16[2048,128]{0,1:T(8,128)(2,1)}), bf16[2048,128]{0,1:T(8,128)(2,1)}) %all-reduce.23.cloned.1.call-update) | async-done | bytes 524304 | tf_op jit(solution)/shard_map/psum | solution.py:33
  504.1 21.5 %all-gather.8 = f32[16,1,128]{2,1,0:T(1,128)S(1)} all-gather(f32[1,1,128]{2,1,0:T(1,128)S(1)} %bitcast.43), channel_id=4, replica_groups=mesh['rows'=16,'cols'=2] {'rows'}, dimensions={0}, use_global_device_ids=true | all-gather | bytes 8704 | tf_op jit(solution)/shard_map/all_gather | solution.py:37
  525.7 11.5 %convolution_bitcast_fusion.2 = f32[3072,128]{1,0:T(8,128)} fusion(bf16[2048,3072]{1,0:T(8,128)(2,1)} %param.3, bf16[2048,128]{0,1:T(8,128)(2,1)} %all-reduce.23.cloned.1.call-done, f32[128]{0:T(128)S(1)} %div.37, bf16[2048,128]{0,1:T(8,128)(2,1)} %all-reduce.19.cloned.1.call-done, bf16[2048,128]{0,1:T(8,128)(2,1)} %all-reduce.15.cloned.1.call-done, ...), kind=kOutput, calls=%fused_computation.2 | convolution fusion | flops 1613496320 | bytes 16254464 | tf_op jit(solution)/shard_map/dot_general | solution.py:10
  537.2 92.1 %all-reduce.25.cloned.1.call-done = f32[3072,128]{1,0:T(8,128)} async-done(((f32[3072,128]{1,0:T(8,128)}), f32[3072,128]{1,0:T(8,128)}) %all-reduce.25.cloned.1.call-update) | async-done | bytes 1572880 | tf_op jit(solution)/shard_map/psum | solution.py:22
  629.3 1.9 multiply_reduce_fusion.2
  631.2 4.9 psum.136
  636.1 2.4 multiply_add_fusion.2
  639.6 10.3 fusion.3
  650.0 27.6 %all-reduce.27.cloned.1.call-done = bf16[2048,128]{0,1:T(8,128)(2,1)} async-done(((bf16[2048,128]{0,1:T(8,128)(2,1)}), bf16[2048,128]{0,1:T(8,128)(2,1)}) %all-reduce.27.cloned.1.call-update) | async-done | bytes 524304 | tf_op jit(solution)/shard_map/psum | solution.py:33
  678.9 21.5 %all-gather.9 = f32[16,1,128]{2,1,0:T(1,128)S(1)} all-gather(f32[1,1,128]{2,1,0:T(1,128)S(1)} %bitcast.44), channel_id=5, replica_groups=mesh['rows'=16,'cols'=2] {'rows'}, dimensions={0}, use_global_device_ids=true | all-gather | bytes 8704 | tf_op jit(solution)/shard_map/all_gather | solution.py:37
  700.5 2.3 fusion.18
  703.7 9.1 convolution_bitcast_fusion.1
  712.9 92.3 %all-reduce.29.cloned.1.call-done = f32[3072,128]{1,0:T(8,128)} async-done(((f32[3072,128]{1,0:T(8,128)}), f32[3072,128]{1,0:T(8,128)}) %all-reduce.29.cloned.1.call-update) | async-done | bytes 1572880 | tf_op jit(solution)/shard_map/psum | solution.py:22
  807.1 4.9 psum.139
  812.0 2.4 multiply_add_fusion.1
  815.5 10.3 fusion.4
  825.9 27.6 %all-reduce.31.cloned.1.call-done = bf16[2048,128]{0,1:T(8,128)(2,1)} async-done(((bf16[2048,128]{0,1:T(8,128)(2,1)}), bf16[2048,128]{0,1:T(8,128)(2,1)}) %all-reduce.31.cloned.1.call-update) | async-done | bytes 524304 | tf_op jit(solution)/shard_map/psum | solution.py:33
  854.8 21.6 %all-gather.10 = f32[16,1,128]{2,1,0:T(1,128)S(1)} all-gather(f32[1,1,128]{2,1,0:T(1,128)S(1)} %bitcast.45), channel_id=6, replica_groups=mesh['rows'=16,'cols'=2] {'rows'}, dimensions={0}, use_global_device_ids=true | all-gather | bytes 8704 | tf_op jit(solution)/shard_map/all_gather | solution.py:37
  876.4 11.3 %convolution_bitcast_fusion = f32[3072,128]{1,0:T(8,128)} fusion(bf16[2048,3072]{1,0:T(8,128)(2,1)} %param.3, f32[2048,128]{0,1:T(8,128)} %copy-done.3, bf16[2048,128]{0,1:T(8,128)(2,1)} %all-reduce.31.cloned.1.call-done, f32[128]{0:T(128)S(1)} %div.41), kind=kOutput, calls=%fused_computation | convolution fusion | flops 1611661312 | bytes 15729152 | tf_op jit(solution)/shard_map/dot_general | solution.py:10
  887.8 92.1 %all-reduce.33.cloned.1.call-done = f32[3072,128]{1,0:T(8,128)} async-done(((f32[3072,128]{1,0:T(8,128)}), f32[3072,128]{1,0:T(8,128)}) %all-reduce.33.cloned.1.call-update) | async-done | bytes 1572880 | tf_op jit(solution)/shard_map/psum | solution.py:22
  981.7 4.9 psum.142
  986.7 2.4 multiply_add_fusion
  990.2 10.3 fusion.5
  1000.9 27.3 %all-reduce.35.cloned.1.call-done = bf16[2048,128]{0,1:T(8,128)(2,1)} async-done(((bf16[2048,128]{0,1:T(8,128)(2,1)}), bf16[2048,128]{0,1:T(8,128)(2,1)}) %all-reduce.35.cloned.1.call-update) | async-done | bytes 524304 | tf_op jit(solution)/shard_map/psum | solution.py:33
  1029.5 21.6 %all-gather.11 = f32[16,1,128]{2,1,0:T(1,128)S(1)} all-gather(f32[1,1,128]{2,1,0:T(1,128)S(1)} %bitcast.46), channel_id=7, replica_groups=mesh['rows'=16,'cols'=2] {'rows'}, dimensions={0}, use_global_device_ids=true | all-gather | bytes 8704 | tf_op jit(solution)/shard_map/all_gather | solution.py:37
  1051.2 2.8 fusion.22
  1054.1 2.5 copy.20
  1056.6 6.5 fusion.6
  1063.1 2.5 copy.19
  (74 shorter events, 22.1 us)
Async XLA Ops:
  7.2 108.2 %all-reduce.13.cloned.1.call-start = ((), (), s32[]{:S(2)}) async-start(), calls=%async_computation | async-start | bytes 3145728 | tf_op jit(solution)/shard_map/psum | solution.py:22
  16.5 98.9 %copy-start.6 = (f32[3072]{0:T(1024)S(1)}, f32[3072]{0:T(1024)}, u32[]{:S(2)}) copy-start(f32[3072]{0:T(1024)} %param.5) | copy-start | bytes 36868
  16.5 138.8 %all-reduce.15.cloned.1.call-start = ((), (), s32[]{:S(2)}) async-start(), calls=%async_computation.1 | async-start | bytes 1048576 | tf_op jit(solution)/shard_map/psum | solution.py:33
  117.2 10.4 copy-start.7
  127.6 153.9 %all-reduce.17.cloned.1.call-start = ((), (), s32[]{:S(2)}) async-start(), calls=%async_computation.2 | async-start | bytes 3145728 | tf_op jit(solution)/shard_map/psum | solution.py:22
  127.9 61.2 %copy-start.5 = (bf16[2048,128]{0,1:T(8,128)(2,1)}, bf16[2048,128]{0,1:T(8,128)(2,1)S(1)}, u32[]{:S(2)}) copy-start(bf16[2048,128]{0,1:T(8,128)(2,1)S(1)} %copy.13) | copy-start | bytes 1572868
  189.1 139.2 %all-reduce.19.cloned.1.call-start = ((), (), s32[]{:S(2)}) async-start(), calls=%async_computation.3 | async-start | bytes 1048576 | tf_op jit(solution)/shard_map/psum | solution.py:33
  300.6 154.5 %all-reduce.21.cloned.1.call-start = ((), (), s32[]{:S(2)}) async-start(), calls=%async_computation.4 | async-start | bytes 3145728 | tf_op jit(solution)/shard_map/psum | solution.py:22
  362.6 140.3 %all-reduce.23.cloned.1.call-start = ((), (), s32[]{:S(2)}) async-start(), calls=%async_computation.5 | async-start | bytes 1048576 | tf_op jit(solution)/shard_map/psum | solution.py:33
  463.7 1.2 copy-start
  475.2 154.1 %all-reduce.25.cloned.1.call-start = ((), (), s32[]{:S(2)}) async-start(), calls=%async_computation.6 | async-start | bytes 3145728 | tf_op jit(solution)/shard_map/psum | solution.py:22
  537.2 140.5 %all-reduce.27.cloned.1.call-start = ((), (), s32[]{:S(2)}) async-start(), calls=%async_computation.7 | async-start | bytes 1048576 | tf_op jit(solution)/shard_map/psum | solution.py:33
  638.5 1.1 copy-start.1
  650.0 155.2 %all-reduce.29.cloned.1.call-start = ((), (), s32[]{:S(2)}) async-start(), calls=%async_computation.8 | async-start | bytes 3145728 | tf_op jit(solution)/shard_map/psum | solution.py:22
  702.8 1.0 copy-start.3
  712.8 140.7 %all-reduce.31.cloned.1.call-start = ((), (), s32[]{:S(2)}) async-start(), calls=%async_computation.9 | async-start | bytes 1048576 | tf_op jit(solution)/shard_map/psum | solution.py:33
  814.4 1.1 copy-start.2
  825.9 154.0 %all-reduce.33.cloned.1.call-start = ((), (), s32[]{:S(2)}) async-start(), calls=%async_computation.10 | async-start | bytes 3145728 | tf_op jit(solution)/shard_map/psum | solution.py:22
  887.7 140.6 %all-reduce.35.cloned.1.call-start = ((), (), s32[]{:S(2)}) async-start(), calls=%async_computation.11 | async-start | bytes 1048576 | tf_op jit(solution)/shard_map/psum | solution.py:33
  989.0 1.2 copy-start.4
Sparse Core Ops, SparseCore 0:
  16.6 98.6 all-reduce.12
  127.7 27.5 all-reduce.14
  189.2 92.2 all-reduce.16
  300.7 27.5 all-reduce.18
  362.7 92.2 all-reduce.20
  475.3 27.5 all-reduce.22
  537.3 91.9 all-reduce.24
  650.1 27.5 all-reduce.26
  713.0 92.2 all-reduce.28
  826.0 27.5 all-reduce.30
  887.8 91.9 all-reduce.32
  1000.7 27.5 all-reduce.34
